TPU v7x, 128 devices: a whole 4x4x4 slice. The times are simulated.
128 devices in a mesh: dp: 32 (over x, z, core), mp: 4 (over y).
Axes of the slice: x: 4, y: 4, z: 4, core: 2. Of those that a mesh axis runs over, the one named last changes fastest.
Arguments:
- partials: bfloat16 [32, 1024, 8192], P('dp', None, 'mp'), may hold values from -11 to 11
- momentum: float32 [128, 256, 256], P(('dp', 'mp')), may hold values from -0.3 to 0.3
- second: float32 [128, 256, 256], P(('dp', 'mp')), may hold values from 0.0002 to 0.02
- left_stat: float32 [128, 256, 256], P(('dp', 'mp')), may hold values from -36 to 36.5, as said below
- right_stat: float32 [128, 256, 256], P(('dp', 'mp')), may hold values from -36 to 36.5, as said below
- left_basis: float32 [128, 256, 256], P(('dp', 'mp')), may hold values from -1 to 1, as said below
- right_basis: float32 [128, 256, 256], P(('dp', 'mp')), may hold values from -1 to 1, as said below
Outputs:
- update: bfloat16 [1024, 8192], P(None, 'mp')
- momentum_new: float32 [128, 256, 256], P(('dp', 'mp'))
- second_new: float32 [128, 256, 256], P(('dp', 'mp'))
- left_new: float32 [128, 256, 256], P(('dp', 'mp'))
- right_new: float32 [128, 256, 256], P(('dp', 'mp'))
- left_basis_new: float32 [128, 256, 256], P(('dp', 'mp'))
- right_basis_new: float32 [128, 256, 256], P(('dp', 'mp'))
Inputs may be any that keep to these rules, and one draw needn't show every extreme that they name: `left_stat`: each block is symmetric positive definite. `right_stat`: each block is symmetric positive definite. `left_basis`: each block is an orthogonal matrix. `right_basis`: each block is an orthogonal matrix.
All inputs are finite; a program needn't handle non-finite values.
Results may differ from a plain program's by a relative error of at most 0.00045.
Values may be sent and summed in bfloat16 or wider, within the bound.
A program may use at most 128 MiB of HBM per device.

v0:
```python
import functools

import jax
import jax.numpy as jnp
from jax import lax
from jax.experimental import pallas as pl
from jax.experimental.pallas import tpu as pltpu
from jax.sharding import Mesh
from jax.sharding import PartitionSpec as P

MESH = pl.DeviceIdType.MESH
HI = lax.Precision.HIGHEST
BLOCK = 256
HALF = 128
NB = 32

beta_first = 0.9
beta_second = 0.95
epsilon = 1e-08


def mm(a, b, ca=1, cb=0):
    return lax.dot_general(
        a, b, (((ca,), (cb,)), ((), ())), precision=HI, preferred_element_type=jnp.float32
    )


def diagonal_inverse(dl, dr, off):
    n = NB // 8
    lane = lax.broadcasted_iota(jnp.int32, (8, 128), 1)
    sub = lax.broadcasted_iota(jnp.int32, (8, 128), 0)
    is_left = lane < 64

    def row(x, s):
        return jnp.broadcast_to(x[s : s + 1, :], (8, 128))

    c = {}
    for j in range(NB):
        for v in range(j // 8, n):
            at_left = jnp.broadcast_to(dl[v][:, off + j : off + j + 1], (8, 128))
            at_right = jnp.broadcast_to(dr[v][:, off + j : off + j + 1], (8, 128))
            c[j, v] = jnp.where(is_left, at_left, at_right)
    lane64 = jnp.bitwise_and(lane, 63)
    x = [jnp.where(lane64 == sub + 8 * v, 1.0, 0.0) for v in range(n)]
    for j in range(NB):
        vj, sj = j // 8, j % 8
        r = lax.rsqrt(row(c[j, vj], sj))
        col = {v: c[j, v] * r for v in range(vj, n)}
        for k in range(j + 1, NB):
            m = row(col[k // 8], k % 8)
            for v in range(k // 8, n):
                c[k, v] = c[k, v] - col[v] * m
        xr = row(x[vj], sj) * r
        x[vj] = jnp.where(sub == sj, xr, jnp.where(sub > sj, x[vj] - col[vj] * xr, x[vj]))
        for v in range(vj + 1, n):
            x[v] = x[v] - col[v] * xr
    return jnp.concatenate(x, axis=0)


def factor_block(k, wl, wr):
    r0 = NB * k
    rows = pl.ds(r0, NB)
    first = 128 * (r0 // 128)
    off = r0 - first
    acc = []
    for w in (wl, wr):
        a = w[rows, first:]
        if k:
            a = a - mm(w[0:r0, first : first + 128], w[0:r0, first:], 0, 0)[off : off + NB]
        acc.append(a)
    groups = [[a[8 * v : 8 * v + 8, 0:128] for v in range(NB // 8)] for a in acc]
    inv = diagonal_inverse(groups[0], groups[1], off)
    for w, a, o in ((wl, acc[0], 0), (wr, acc[1], 64)):
        w[rows, first:] = mm(inv[:, o : o + NB], a)


def kernel(
    nx, nz, ny, part, mom, sec, lstat, rstat, lbas, rbas,
    upd, mom_o, sec_o, ln_o, rn_o, lb_o, rb_o,
    state, res, own, r1, pair, rsib, r2, g_ref, tmp, wl, wr, nsend, nrecv, nsum, ysend, yrecv, ublk, gath,
    s_state, s_res, s_own, s1s, s1r, sbs, sbr, s2s, s2r, nps, npr, nys, nyr, a1s, a1r, a2s, a2r, abs_, abr, s_out,
):
    x, z, c, y = (lax.axis_index(a) for a in ("x", "z", "c", "y"))
    n = (nx, nz)
    pos = (x, z)
    sib = (x, z, 1 - c, y)

    def peer(axis, d):
        return ((x + d) % nx, z, c, y) if axis == 0 else (x, (z + d) % nz, c, y)

    def ypeer(d):
        return (x, z, c, (y + d) % ny)

    def rdma(src, dst, ss, rs, dev):
        return pltpu.make_async_remote_copy(
            src_ref=src, dst_ref=dst, send_sem=ss, recv_sem=rs, device_id=dev, device_id_type=MESH
        )

    loads = [
        pltpu.make_async_copy(src, state.at[i], s_state.at[i])
        for i, src in enumerate((mom, sec, lstat, rstat, lbas, rbas))
    ]

    def slab(h, bx, bz):
        return part.at[bx, HALF * h : HALF * (h + 1), pl.ds(pl.multiple_of(512 * bz, 512), 512)]

    def chunk(h, d, e):
        if h == 0:
            return slab(0, (x + d) % nx, (z + e) % nz)
        return slab(1, (x + e) % nx, (z + d) % nz)

    order = {h: [e for e in (2, 1, 3) if e < n[1 - h]] + [0] for h in (0, 1)}
    dist = {h: [d for d in (2, 1, 3) if d < n[h]] for h in (0, 1)}
    own_copies = {
        (h, e): pltpu.make_async_copy(chunk(h, 0, e), own.at[h, e], s_own.at[h, e])
        for h in (0, 1)
        for e in order[h]
    }

    barrier = pltpu.get_barrier_semaphore()
    hello = [peer(a, d) for a in (0, 1) for d in range(1, n[a])] + [ypeer(d) for d in range(1, ny)] + [sib]
    for dev in hello:
        pl.semaphore_signal(barrier, inc=1, device_id=dev, device_id_type=MESH)
    for q in own_copies.values():
        q.start()
    for q in loads:
        q.start()
    pl.semaphore_wait(barrier, len(hello))

    phase1 = {}
    for e in range(max(nx, nz)):
        for h in (0, 1):
            if e < len(order[h]):
                ee = order[h][e]
                for d in dist[h]:
                    q = rdma(
                        chunk(h, d, ee), r1.at[h, d - 1, ee], s1s.at[h, d - 1, ee], s1r.at[h, d - 1, ee], peer(h, d)
                    )
                    q.start()
                    phase1[h, d, ee] = q

    for q in loads:
        q.wait()
    lb, rb = state[4], state[5]
    tmp[0] = beta_second * mm(lb, state[2], 0, 0)
    tmp[1] = beta_second * mm(rb, state[3], 0, 0)
    tmp[2] = beta_first * mm(mm(lb, state[0], 0, 0), rb)

    sibling, phase2 = {}, {}

    def pass_on(h, e):
        q = sibling[h, e]
        q.wait_recv()
        pair[h, c, e] = pair[h, c, e] + rsib[h, e]
        if e:
            q = rdma(pair.at[h, c, e], r2.at[h, e - 1], s2s.at[h, e - 1], s2r.at[h, e - 1], peer(1 - h, e))
            q.start()
            phase2[h, e] = q

    steps = max(len(order[0]), len(order[1]))
    for i in range(steps + 1):
        for h in (0, 1):
            if i < len(order[h]):
                e = order[h][i]
                own_copies[h, e].wait()
                for d in dist[h]:
                    phase1[h, d, e].wait_recv()
                total = own[h, e].astype(jnp.float32)
                for d in range(1, n[h]):
                    total = total + r1[h, d - 1, e].astype(jnp.float32)
                pair[h, 0, e] = total[:, :BLOCK]
                pair[h, 1, e] = total[:, BLOCK:]
                q = rdma(pair.at[h, 1 - c, e], rsib.at[h, e], sbs.at[h, e], sbr.at[h, e], sib)
                q.start()
                sibling[h, e] = q
        for h in (0, 1):
            if 1 <= i <= len(order[h]):
                pass_on(h, order[h][i - 1])
    for h in (0, 1):
        total = pair[h, c, 0]
        for e in dist[1 - h]:
            phase2[h, e].wait_recv()
            total = total + r2[h, e - 1]
        g_ref[HALF * h : HALF * (h + 1), :] = total

    g = g_ref[...]
    t1 = mm(lb, g, 0, 0)
    rot = mm(t1, rb)
    second_new = beta_second * state[1] + (1.0 - beta_second) * rot * rot
    direction = (tmp[2] + (1.0 - beta_first) * rot) / (jnp.sqrt(second_new) + epsilon)
    res[1] = second_new

    def folded(v):
        s = jnp.sum(v * v, axis=0, keepdims=True)
        return s[:, :128] + s[:, 128:]

    nsend[0:1, :] = folded(g)
    nsend[1:2, :] = folded(direction)
    members = 2 * nx * nz
    me = (x * nz + z) * 2 + c
    plane = []
    for k in range(1, members):
        to = (me + k) % members
        dev = (to // (2 * nz), (to // 2) % nz, to % 2, y)
        q = rdma(nsend, nrecv.at[k - 1], nps.at[k - 1], npr.at[k - 1], dev)
        q.start()
        plane.append(q)

    tmp[2] = mm(mm(lb, direction), rb, 1, 1)
    t2 = mm(g, rb)
    pl_t = tmp[0] + (1.0 - beta_second) * mm(t1, g, 1, 1)
    pr_t = tmp[1] + (1.0 - beta_second) * mm(t2, g, 0, 0)
    wl[:, BLOCK:] = pl_t
    wr[:, BLOCK:] = pr_t
    wl[:, :BLOCK] = mm(pl_t, pl_t, 1, 1)
    wr[:, :BLOCK] = mm(pr_t, pr_t, 1, 1)
    res[0] = beta_first * state[0] + (1.0 - beta_first) * g
    res[2] = beta_second * state[2] + (1.0 - beta_second) * mm(g, g, 1, 1)
    res[3] = beta_second * state[3] + (1.0 - beta_second) * mm(g, g, 0, 0)
    stores = [
        pltpu.make_async_copy(res.at[i], dst, s_res.at[i])
        for i, dst in enumerate((mom_o, sec_o, ln_o, rn_o, lb_o, rb_o))
    ]
    for q in stores[:4]:
        q.start()

    blocks = BLOCK // NB
    factor_block(0, wl, wr)

    for q in plane:
        q.wait_recv()
    total = nsend[...]
    for k in range(members - 1):
        total = total + nrecv[k]
    ysend[...] = total
    along_y = []
    for d in range(1, ny):
        q = rdma(ysend, yrecv.at[d - 1], nys.at[d - 1], nyr.at[d - 1], ypeer(d))
        q.start()
        along_y.append(q)

    factor_block(1, wl, wr)
    factor_block(2, wl, wr)

    for q in along_y:
        q.wait_recv()
    total = ysend[...]
    for d in range(1, ny):
        total = total + yrecv[d - 1]
    sums = jnp.sum(total, axis=1, keepdims=True)
    scale = jnp.sqrt(sums[0:1, :] / sums[1:2, :])
    ublk[...] = (tmp[2] * scale).astype(jnp.bfloat16)

    def place(h, bx, bz):
        return upd.at[bx, HALF * h : HALF * (h + 1), pl.ds(pl.multiple_of(512 * bz + 256 * c, 256), 256)]

    def held(h, s):
        return ublk.at[HALF * h : HALF * (h + 1), :] if s == 0 else gath.at[h, s - 1]

    def source(h, s):
        return place(h, x, (z + nz - s) % nz) if h == 0 else place(h, (x + nx - s) % nx, z)

    def arrived(h, d, s):
        if h == 0:
            return place(h, (x + nx - d) % nx, (z + nz - s) % nz)
        return place(h, (x + nx - s) % nx, (z + nz - d) % nz)

    ag1, ag2, to_sib, local = {}, {}, [], []

    def forward(h, s):
        for d in dist[h]:
            q = rdma(held(h, s), source(h, s), a2s.at[h, d - 1, s], a2r.at[h, d - 1, s], peer(h, d))
            q.start()
            ag2[h, d, s] = q
        i = len(to_sib)
        q = rdma(held(h, s), source(h, s), abs_.at[i], abr.at[i], sib)
        q.start()
        to_sib.append(q)
        q = pltpu.make_async_copy(held(h, s), source(h, s), s_out.at[h, s])
        q.start()
        local.append(q)

    for h in (0, 1):
        for d in dist[1 - h]:
            q = rdma(held(h, 0), gath.at[h, d - 1], a1s.at[h, d - 1], a1r.at[h, d - 1], peer(1 - h, d))
            q.start()
            ag1[h, d] = q
    for h in (0, 1):
        forward(h, 0)

    factor_block(3, wl, wr)
    factor_block(4, wl, wr)

    for s in (1, 3, 2):
        for h in (0, 1):
            if s < n[1 - h]:
                ag1[h, s].wait_recv()
                forward(h, s)

    for k in range(5, blocks):
        factor_block(k, wl, wr)
    res[4] = wl[:, BLOCK:].T
    res[5] = wr[:, BLOCK:].T
    for q in stores[4:]:
        q.start()

    for s in (0, 1, 3, 2):
        for d in (1, 3, 2):
            for h in (0, 1):
                if d < n[h] and s < n[1 - h]:
                    ag2[h, d, s].wait_recv()
                    i = len(to_sib)
                    q = rdma(arrived(h, d, s), arrived(h, d, s), abs_.at[i], abr.at[i], sib)
                    q.start()
                    to_sib.append(q)

    for q in to_sib:
        q.wait_recv()
    for q in local + stores:
        q.wait()
    for group in (phase1, sibling, phase2, ag1, ag2):
        for q in group.values():
            q.wait_send()
    for q in plane + along_y + to_sib:
        q.wait_send()


def on_device(nx, nz, ny, partials, *states):
    f32, bf16 = jnp.float32, jnp.bfloat16
    rows, width = partials.shape[1:]
    part = partials.reshape(nx, BLOCK, width)
    hbm = pl.BlockSpec(memory_space=pl.ANY)
    ring = max(nx, nz)
    square = (BLOCK, BLOCK)
    dma = pltpu.SemaphoreType.DMA
    members = 2 * nx * nz
    blocks = 2 * nx * nz
    outs = pl.pallas_call(
        functools.partial(kernel, nx, nz, ny),
        out_shape=[jax.ShapeDtypeStruct((nx, BLOCK, width), bf16)] + [jax.ShapeDtypeStruct(square, f32)] * 6,
        in_specs=[hbm] * 7,
        out_specs=[hbm] * 7,
        scratch_shapes=[
            pltpu.VMEM((6, *square), f32),
            pltpu.VMEM((6, *square), f32),
            pltpu.VMEM((2, ring, HALF, 2 * BLOCK), bf16),
            pltpu.VMEM((2, ring - 1, ring, HALF, 2 * BLOCK), bf16),
            pltpu.VMEM((2, 2, ring, HALF, BLOCK), f32),
            pltpu.VMEM((2, ring, HALF, BLOCK), f32),
            pltpu.VMEM((2, ring - 1, HALF, BLOCK), f32),
            pltpu.VMEM(square, f32),
            pltpu.VMEM((3, *square), f32),
            pltpu.VMEM((BLOCK, 2 * BLOCK), f32),
            pltpu.VMEM((BLOCK, 2 * BLOCK), f32),
            pltpu.VMEM((2, 128), f32),
            pltpu.VMEM((members - 1, 2, 128), f32),
            pltpu.VMEM((2, 128), f32),
            pltpu.VMEM((2, 128), f32),
            pltpu.VMEM((ny - 1, 2, 128), f32),
            pltpu.VMEM(square, bf16),
            pltpu.VMEM((2, ring - 1, HALF, BLOCK), bf16),
            dma((6,)), dma((6,)), dma((2, ring)),
            dma((2, ring - 1, ring)), dma((2, ring - 1, ring)),
            dma((2, ring)), dma((2, ring)),
            dma((2, ring - 1)), dma((2, ring - 1)),
            dma((members - 1,)), dma((members - 1,)),
            dma((ny - 1,)), dma((ny - 1,)),
            dma((2, ring - 1)), dma((2, ring - 1)),
            dma((2, ring - 1, ring)), dma((2, ring - 1, ring)),
            dma((blocks,)), dma((blocks,)),
            dma((2, ring)),
        ],
        compiler_params=pltpu.CompilerParams(
            collective_id=0, has_side_effects=True, vmem_limit_bytes=48 * 1024 * 1024
        ),
    )(part, *(s[0] for s in states))
    return (outs[0].reshape(rows, width), *(o[None] for o in outs[1:]))


def solution(mesh):
    nx = nz = 4
    ny = mesh.shape["mp"]
    split = Mesh(mesh.devices.reshape(nx, nz, 2, ny), ("x", "z", "c", "y"))
    dp = ("x", "z", "c")
    whole = P(dp + ("y",), None, None)
    return jax.shard_map(
        functools.partial(on_device, nx, nz, ny),
        mesh=split,
        in_specs=(P(dp, None, "y"),) + (whole,) * 6,
        out_specs=(P(None, "y"),) + (whole,) * 6,
        check_vma=False,
    )
```

profile of v0, /device:TPU:1, one launch (start us, length us, event | category | flops | bytes accessed | tf_op | source)
XLA Modules:
  0.0 85.6 jit_solution(7985896117695821257)
XLA Ops:
  0.6 0.0 copy-start
  0.6 0.9 %copy-done = f32[1,256,256]{2,1,0:T(8,128)S(1)} copy-done((f32[1,256,256]{2,1,0:T(8,128)S(1)}, f32[1,256,256]{2,1,0:T(8,128)}, u32[]{:S(2)}) %copy-start) | copy-done | bytes 262168
  1.6 0.0 copy-start.1
  1.6 0.9 %copy-done.1 = f32[1,256,256]{2,1,0:T(8,128)S(1)} copy-done((f32[1,256,256]{2,1,0:T(8,128)S(1)}, f32[1,256,256]{2,1,0:T(8,128)}, u32[]{:S(2)}) %copy-start.1) | copy-done | bytes 262168
  2.5 0.0 copy-start.2
  2.5 0.9 %copy-done.2 = f32[1,256,256]{2,1,0:T(8,128)S(1)} copy-done((f32[1,256,256]{2,1,0:T(8,128)S(1)}, f32[1,256,256]{2,1,0:T(8,128)}, u32[]{:S(2)}) %copy-start.2) | copy-done | bytes 262168
  3.5 0.0 copy-start.3
  3.5 0.9 %copy-done.3 = f32[1,256,256]{2,1,0:T(8,128)S(1)} copy-done((f32[1,256,256]{2,1,0:T(8,128)S(1)}, f32[1,256,256]{2,1,0:T(8,128)}, u32[]{:S(2)}) %copy-start.3) | copy-done | bytes 262168
  4.4 0.0 copy-start.4
  4.4 0.9 %copy-done.4 = f32[1,256,256]{2,1,0:T(8,128)S(1)} copy-done((f32[1,256,256]{2,1,0:T(8,128)S(1)}, f32[1,256,256]{2,1,0:T(8,128)}, u32[]{:S(2)}) %copy-start.4) | copy-done | bytes 262168
  5.4 0.0 copy-start.5
  5.4 0.9 %copy-done.5 = f32[1,256,256]{2,1,0:T(8,128)S(1)} copy-done((f32[1,256,256]{2,1,0:T(8,128)S(1)}, f32[1,256,256]{2,1,0:T(8,128)}, u32[]{:S(2)}) %copy-start.5) | copy-done | bytes 262168
  6.3 70.2 %shard_map.126 = (bf16[4,256,2048]{2,1,0:T(8,128)(2,1)}, f32[256,256]{1,0:T(8,128)S(1)}, f32[256,256]{1,0:T(8,128)S(1)}, f32[256,256]{1,0:T(8,128)S(1)}, f32[256...) custom-call(bf16[4,256,2048]{2,1,0:T(8,128)(2,1)} %bitcast.26, f32[256,256]{1,0:T(8,128)S(1)} %bitcast.14, ...), custom_call_target="tpu_custom_call" | custom-call | tf_op jit(solution)/shard_map/pallas_call | solution.py:338
  76.6 4.8 %copy.21 = bf16[1024,2048]{1,0:T(8,128)(2,1)} copy(bf16[1024,2048]{1,0:T(8,128)(2,1)} %bitcast.27) | data formatting | bytes 8388608
  81.3 0.7 copy.22
  82.0 0.7 copy.23
  82.7 0.7 copy.24
  83.4 0.7 copy.25
  84.2 0.7 copy.26
  84.9 0.7 copy.27
Async XLA Ops:
  0.6 1.0 %copy-start = (f32[1,256,256]{2,1,0:T(8,128)S(1)}, f32[1,256,256]{2,1,0:T(8,128)}, u32[]{:S(2)}) copy-start(f32[1,256,256]{2,1,0:T(8,128)} %param.8) | copy-start | bytes 786436
  1.6 0.9 %copy-start.1 = (f32[1,256,256]{2,1,0:T(8,128)S(1)}, f32[1,256,256]{2,1,0:T(8,128)}, u32[]{:S(2)}) copy-start(f32[1,256,256]{2,1,0:T(8,128)} %param.9) | copy-start | bytes 786436
  2.5 0.9 %copy-start.2 = (f32[1,256,256]{2,1,0:T(8,128)S(1)}, f32[1,256,256]{2,1,0:T(8,128)}, u32[]{:S(2)}) copy-start(f32[1,256,256]{2,1,0:T(8,128)} %param.10) | copy-start | bytes 786436
  3.5 0.9 %copy-start.3 = (f32[1,256,256]{2,1,0:T(8,128)S(1)}, f32[1,256,256]{2,1,0:T(8,128)}, u32[]{:S(2)}) copy-start(f32[1,256,256]{2,1,0:T(8,128)} %param.11) | copy-start | bytes 786436
  4.4 0.9 %copy-start.4 = (f32[1,256,256]{2,1,0:T(8,128)S(1)}, f32[1,256,256]{2,1,0:T(8,128)}, u32[]{:S(2)}) copy-start(f32[1,256,256]{2,1,0:T(8,128)} %param.12) | copy-start | bytes 786436
  5.4 0.9 %copy-start.5 = (f32[1,256,256]{2,1,0:T(8,128)S(1)}, f32[1,256,256]{2,1,0:T(8,128)}, u32[]{:S(2)}) copy-start(f32[1,256,256]{2,1,0:T(8,128)} %param.13) | copy-start | bytes 786436
where the time goes:
time: 85.9 us; the launch traced here: 85.6 us
  Pallas kernels  70.2 us (82%)
  local copies, waits for them, and re-layouts  14.7 us (17%)
    pallas_call x1, Pallas kernels, on_device(): pl.pallas_call(functools.partial(kernel, nx, nz, ny), out_shape=[jax.Shap...  70.2 us
    unnamed x19, local copies, waits for them, and re-layouts  14.7 us

commit v1 on v0

v1 whole, which is shorter than its diff:
```python
import functools

import jax
import jax.numpy as jnp
from jax import lax
from jax.experimental import pallas as pl
from jax.experimental.pallas import tpu as pltpu
from jax.sharding import Mesh
from jax.sharding import PartitionSpec as P

MESH = pl.DeviceIdType.MESH
HI = lax.Precision.HIGHEST
BLOCK = 256
HALF = 128
NB = 32
EARLY = 3

beta_first = 0.9
beta_second = 0.95
epsilon = 1e-08


def mm(a, b, ca=1, cb=0):
    return lax.dot_general(
        a, b, (((ca,), (cb,)), ((), ())), precision=HI, preferred_element_type=jnp.float32
    )


def parts(a):
    high = a.astype(jnp.bfloat16)
    return high, (a - high.astype(jnp.float32)).astype(jnp.bfloat16)


def mm3(a, b, ca=1, cb=0):
    dot = lambda u, v: lax.dot_general(u, v, (((ca,), (cb,)), ((), ())), preferred_element_type=jnp.float32)
    return dot(a[0], b[0]) + (dot(a[0], b[1]) + dot(a[1], b[0]))


def diagonal_inverse(dl, dr, off):
    n = NB // 8
    lane = lax.broadcasted_iota(jnp.int32, (8, 128), 1)
    sub = lax.broadcasted_iota(jnp.int32, (8, 128), 0)
    is_left = lane < 64

    def row(x, s):
        return jnp.broadcast_to(x[s : s + 1, :], (8, 128))

    c = {}
    for j in range(NB):
        for v in range(j // 8, n):
            at_left = jnp.broadcast_to(dl[v][:, off + j : off + j + 1], (8, 128))
            at_right = jnp.broadcast_to(dr[v][:, off + j : off + j + 1], (8, 128))
            c[j, v] = jnp.where(is_left, at_left, at_right)
    lane64 = jnp.bitwise_and(lane, 63)
    x = [jnp.where(lane64 == sub + 8 * v, 1.0, 0.0) for v in range(n)]
    for j in range(NB):
        vj, sj = j // 8, j % 8
        r = lax.rsqrt(row(c[j, vj], sj))
        col = {v: c[j, v] * r for v in range(vj, n)}
        for k in range(j + 1, NB):
            m = row(col[k // 8], k % 8)
            for v in range(k // 8, n):
                c[k, v] = c[k, v] - col[v] * m
        xr = row(x[vj], sj) * r
        x[vj] = jnp.where(sub == sj, xr, jnp.where(sub > sj, x[vj] - col[vj] * xr, x[vj]))
        for v in range(vj + 1, n):
            x[v] = x[v] - col[v] * xr
    return jnp.concatenate(x, axis=0)


def factor_block(k, wl, wr):
    r0 = NB * k
    rows = pl.ds(r0, NB)
    first = 128 * (r0 // 128)
    off = r0 - first
    acc = []
    for w in (wl, wr):
        a = w[rows, first:]
        if k:
            a = a - mm(w[0:r0, first : first + 128], w[0:r0, first:], 0, 0)[off : off + NB]
        acc.append(a)
    groups = [[a[8 * v : 8 * v + 8, 0:128] for v in range(NB // 8)] for a in acc]
    inv = diagonal_inverse(groups[0], groups[1], off)
    for w, a, o in ((wl, acc[0], 0), (wr, acc[1], 64)):
        w[rows, first:] = mm(inv[:, o : o + NB], a)


def kernel(
    nx, nz, ny, part, mom, sec, lstat, rstat, lbas, rbas,
    upd, mom_o, sec_o, ln_o, rn_o, lb_o, rb_o,
    state, own, r1, pair, rsib, r2, g_ref, tmp, wl, wr, nsend, nrecv,
    s_state, s_own, s1s, s1r, sbs, sbr, s2s, s2r, nps, npr, a1s, a1r, a2s, a2r, abs_, abr,
):
    x, z, c, y = (lax.axis_index(a) for a in ("x", "z", "c", "y"))
    n = (nx, nz)
    xs = [x] + [(x + d) % nx for d in range(1, nx)]
    zs = [z] + [(z + d) % nz for d in range(1, nz)]
    ys = [y] + [(y + d) % ny for d in range(1, ny)]
    cs = [c, 1 - c]
    sib = (x, z, cs[1], y)

    def peer(axis, d):
        return (xs[d], z, c, y) if axis == 0 else (x, zs[d], c, y)

    def rdma(src, dst, ss, rs, dev):
        return pltpu.make_async_remote_copy(
            src_ref=src, dst_ref=dst, send_sem=ss, recv_sem=rs, device_id=dev, device_id_type=MESH
        )

    def bytes_of(ref, sem):
        pltpu.make_async_copy(ref, ref, sem).wait()

    loads = [
        pltpu.make_async_copy(src, state.at[i], s_state.at[i])
        for i, src in enumerate((mom, sec, lstat, rstat, lbas, rbas))
    ]

    def slab(h, bx, bz):
        return part.at[bx, HALF * h : HALF * (h + 1), pl.ds(pl.multiple_of(512 * bz, 512), 512)]

    def chunk(h, d, e):
        return slab(0, xs[d], zs[e]) if h == 0 else slab(1, xs[e], zs[d])

    order = {h: [e for e in (2, 1, 3) if e < n[1 - h]] + [0] for h in (0, 1)}
    dist = {h: [d for d in (2, 1, 3) if d < n[h]] for h in (0, 1)}
    own_copies = {
        (h, e): pltpu.make_async_copy(chunk(h, 0, e), own.at[h, e], s_own.at[h, e])
        for h in (0, 1)
        for e in order[h]
    }

    barrier = pltpu.get_barrier_semaphore()
    hello = [peer(a, d) for a in (0, 1) for d in range(1, n[a])] + [(x, z, c, v) for v in ys[1:]] + [sib]
    for dev in hello:
        pl.semaphore_signal(barrier, inc=1, device_id=dev, device_id_type=MESH)
    for q in own_copies.values():
        q.start()
    for q in loads:
        q.start()
    pl.semaphore_wait(barrier, len(hello))

    for i in range(max(nx, nz)):
        for h in (0, 1):
            if i < len(order[h]):
                e = order[h][i]
                for d in dist[h]:
                    rdma(chunk(h, d, e), r1.at[h, e, d - 1], s1s.at[0], s1r.at[h, e], peer(h, d)).start()

    for q in loads:
        q.wait()
    lb, rb = state[4], state[5]
    lbt, rbt = lb.T, rb.T
    tmp[0] = beta_second * mm(lbt, state[2])
    tmp[1] = beta_second * mm(rbt, state[3])
    tmp[2] = beta_first * mm(mm(lbt, state[0]), rb)
    tmp[3] = lbt
    tmp[4] = rbt

    def pass_on(h, e):
        bytes_of(rsib.at[h, e], sbr.at[h, e])
        pair[h, c, e] = pair[h, c, e] + rsib[h, e]
        if e:
            rdma(pair.at[h, c, e], r2.at[h, e - 1], s2s.at[0], s2r.at[h], peer(1 - h, e)).start()

    for i in range(max(nx, nz) + 1):
        for h in (0, 1):
            if i < len(order[h]):
                e = order[h][i]
                own_copies[h, e].wait()
                bytes_of(r1.at[h, e], s1r.at[h, e])
                total = own[h, e].astype(jnp.float32)
                for d in range(1, n[h]):
                    total = total + r1[h, e, d - 1].astype(jnp.float32)
                pair[h, 0, e] = total[:, :BLOCK]
                pair[h, 1, e] = total[:, BLOCK:]
                rdma(pair.at[h, cs[1], e], rsib.at[h, e], sbs.at[0], sbr.at[h, e], sib).start()
        for h in (0, 1):
            if 1 <= i <= len(order[h]):
                pass_on(h, order[h][i - 1])
    for h in (0, 1):
        total = pair[h, c, 0]
        bytes_of(r2.at[h], s2r.at[h])
        for e in range(1, n[1 - h]):
            total = total + r2[h, e - 1]
        g_ref[HALF * h : HALF * (h + 1), :] = total

    g = g_ref[...]
    gp, rbp = parts(g), parts(rb)
    t1p = parts(mm3(parts(tmp[3]), gp))
    rot = mm3(t1p, rbp)
    second_new = beta_second * state[1] + (1.0 - beta_second) * rot * rot
    direction = (tmp[2] + (1.0 - beta_first) * rot) / (jnp.sqrt(second_new) + epsilon)
    sec_o[...] = second_new

    def folded(v):
        s = jnp.sum(v * v, axis=0, keepdims=True)
        s = s[:, :128] + s[:, 128:]
        return s + pltpu.roll(s, 64, 1)

    is_grad = lax.broadcasted_iota(jnp.int32, (1, 128), 1) < 64
    mine = jnp.where(is_grad, folded(g), folded(direction))
    nsend[...] = mine
    others = 2 * nx * nz * ny - 1
    for dx in range(nx):
        for dz in range(nz):
            for dc in range(2):
                for dy in range(ny):
                    k = ((dx * nz + dz) * 2 + dc) * ny + dy
                    if k:
                        dev = (xs[dx], zs[dz], cs[dc], ys[dy])
                        rdma(nsend, nrecv.at[k - 1 : k, :], nps.at[0], npr.at[0], dev).start()

    tmp[2] = mm3(parts(mm3(parts(lb), parts(direction))), rbp, 1, 1)
    t2p = parts(mm3(parts(tmp[4]), gp, 1, 1))
    pl_t = tmp[0] + (1.0 - beta_second) * mm3(t1p, gp, 1, 1)
    pr_t = tmp[1] + (1.0 - beta_second) * mm3(t2p, gp)
    wl[:, BLOCK:] = pl_t
    wr[:, BLOCK:] = pr_t
    wl[:, :BLOCK] = mm(pl_t, pl_t, 1, 1)
    wr[:, :BLOCK] = mm(pr_t, pr_t, 1, 1)
    for k in range(EARLY):
        factor_block(k, wl, wr)

    bytes_of(nrecv.at[0:others, :], npr.at[0])
    total = jnp.sum(nrecv[0:others, :], axis=0, keepdims=True) + mine
    grad_norm = jnp.sum(jnp.where(is_grad, total, 0.0), axis=1, keepdims=True)
    step_norm = jnp.sum(jnp.where(is_grad, 0.0, total), axis=1, keepdims=True)
    update = (tmp[2] * jnp.sqrt(grad_norm / step_norm)).astype(jnp.bfloat16)
    columns = pl.ds(pl.multiple_of(512 * z + 256 * c, 256), 256)
    upd[x, :, columns] = update

    def place(h, bx, bz):
        return upd.at[bx, HALF * h : HALF * (h + 1), pl.ds(pl.multiple_of(512 * bz + 256 * c, 256), 256)]

    def spot(h, d, s):
        back = lambda v, k, m: v[(m - k) % m]
        return place(h, back(xs, d, nx), back(zs, s, nz)) if h == 0 else place(h, back(xs, s, nx), back(zs, d, nz))

    def send(where, ss, rs, dev):
        rdma(where, where, ss, rs, dev).start()

    def arrive(where, rs):
        bytes_of(where, rs)

    def share(h, d, s):
        send(spot(h, d, s), abs_.at[0], abr.at[0], sib)

    def start(h):
        for d in (1, 3, 2):
            send(spot(h, 0, 0), a1s.at[0], a1r.at[h, d - 1], peer(1 - h, d))

    def onward(h, s):
        if s:
            arrive(spot(h, 0, s), a1r.at[h, s - 1])
        for d in (2, 1, 3) if s == 2 else (1, 3):
            send(spot(h, 0, s), a2s.at[0], a2r.at[h, d - 1, s], peer(h, d))
        share(h, 0, s)

    ways = {0: 1, 1: 3, 3: 1}

    def relay(h, s):
        for d in (1, 3):
            arrive(spot(h, d, s), a2r.at[h, d - 1, s])
            if ways.get(s) == d:
                send(spot(h, d, s), a2s.at[0], a2r.at[h, 1, s], peer(h, d))
            share(h, d, s)

    def last(h, s):
        arrive(spot(h, 2, s), a2r.at[h, 1, s])
        share(h, 2, s)

    both = lambda f, *a: [f(h, *a) for h in (0, 1)]
    both(start)
    both(onward, 0)

    def rest_of_products():
        mom_o[...] = beta_first * state[0] + (1.0 - beta_first) * g_ref[...]
        q = parts(g_ref[...])
        ln_o[...] = beta_second * state[2] + (1.0 - beta_second) * mm3(q, q, 1, 1)
        qt = parts(g_ref[...].T)
        rn_o[...] = beta_second * state[3] + (1.0 - beta_second) * mm3(qt, q)

    def bases():
        lb_o[...] = wl[:, BLOCK:].T
        rb_o[...] = wr[:, BLOCK:].T

    work = [functools.partial(factor_block, k, wl, wr) for k in range(EARLY, BLOCK // NB)]
    work = work + [rest_of_products, bases]
    polls = {
        1: ((onward, 1), (onward, 3)),
        2: ((relay, 0), (onward, 2)),
        3: ((relay, 1),),
        4: ((last, 0), (relay, 3)),
        5: ((last, 1), (relay, 2)),
        len(work) - 1: ((last, 3), (last, 2)),
    }
    for i, do in enumerate(work):
        do()
        for q in polls.get(i, ()):
            both(*q)

    bytes_of(upd.at[0:2], abr.at[0])
    bytes_of(r1, s1s.at[0])
    bytes_of(rsib, sbs.at[0])
    bytes_of(r2, s2s.at[0])
    bytes_of(nrecv.at[0:others, :], nps.at[0])
    bytes_of(upd.at[0, 0:192, 0:1024], a1s.at[0])
    bytes_of(upd.at[0:3, 0:128, :], a2s.at[0])
    bytes_of(upd.at[0:2], abs_.at[0])


def store_kernel(*refs):
    m = len(refs) // 2
    sem = refs[-1]
    copies = [pltpu.make_async_copy(refs[i], refs[m + i], sem.at[i]) for i in range(m)]
    for q in copies:
        q.start()
    for q in copies:
        q.wait()


def on_device(nx, nz, ny, partials, *states):
    f32, bf16 = jnp.float32, jnp.bfloat16
    rows, width = partials.shape[1:]
    part = partials.reshape(nx, BLOCK, width)
    hbm = pl.BlockSpec(memory_space=pltpu.HBM)
    vmem = pl.BlockSpec(memory_space=pltpu.VMEM)
    ring = max(nx, nz)
    square = (BLOCK, BLOCK)
    dma = pltpu.SemaphoreType.DMA
    members = 2 * nx * nz
    shapes = [jax.ShapeDtypeStruct((nx, BLOCK, width), bf16)] + [jax.ShapeDtypeStruct(square, f32)] * 6
    outs = pl.pallas_call(
        functools.partial(kernel, nx, nz, ny),
        out_shape=shapes,
        in_specs=[hbm] * 7,
        out_specs=[vmem] * 7,
        scratch_shapes=[
            pltpu.VMEM((6, *square), f32),
            pltpu.VMEM((2, ring, HALF, 2 * BLOCK), bf16),
            pltpu.VMEM((2, ring, ring - 1, HALF, 2 * BLOCK), bf16),
            pltpu.VMEM((2, 2, ring, HALF, BLOCK), f32),
            pltpu.VMEM((2, ring, HALF, BLOCK), f32),
            pltpu.VMEM((2, ring - 1, HALF, BLOCK), f32),
            pltpu.VMEM(square, f32),
            pltpu.VMEM((5, *square), f32),
            pltpu.VMEM((BLOCK, 2 * BLOCK), f32),
            pltpu.VMEM((BLOCK, 2 * BLOCK), f32),
            pltpu.VMEM((1, 128), f32),
            pltpu.VMEM((members * ny, 128), f32),
            dma((6,)), dma((2, ring)),
            dma((1,)), dma((2, ring)),
            dma((1,)), dma((2, ring)),
            dma((1,)), dma((2,)),
            dma((1,)), dma((1,)),
            dma((1,)), dma((2, ring - 1)),
            dma((1,)), dma((2, ring - 1, ring)),
            dma((1,)), dma((1,)),
        ],
        compiler_params=pltpu.CompilerParams(
            collective_id=0, has_side_effects=True, vmem_limit_bytes=36 * 1024 * 1024
        ),
    )(*(pltpu.with_memory_space_constraint(a, pltpu.HBM) for a in (part, *(s[0] for s in states))))
    outs = pl.pallas_call(
        store_kernel,
        out_shape=shapes,
        in_specs=[vmem] * 7,
        out_specs=[hbm] * 7,
        scratch_shapes=[dma((7,))],
        compiler_params=pltpu.CompilerParams(vmem_limit_bytes=8 * 1024 * 1024),
    )(*outs)
    return (outs[0].reshape(rows, width), *(o[None] for o in outs[1:]))


def solution(mesh):
    nx = nz = 4
    ny = mesh.shape["mp"]
    split = Mesh(mesh.devices.reshape(nx, nz, 2, ny), ("x", "z", "c", "y"))
    dp = ("x", "z", "c")
    whole = P(dp + ("y",), None, None)
    return jax.shard_map(
        functools.partial(on_device, nx, nz, ny),
        mesh=split,
        in_specs=(P(dp, None, "y"),) + (whole,) * 6,
        out_specs=(P(None, "y"),) + (whole,) * 6,
        check_vma=False,
    )
```

time: 85.9 us -> 74.1 us (0.86)
  local copies, waits for them, and re-layouts: 14.7 us -> 0 us
  Pallas kernels: 70.2 us -> 73.4 us
    unnamed x19 -> x0, local copies, waits for them, and re-layouts: 14.7 us -> none
    pallas_call x1 -> x2, Pallas kernels: 70.2 us -> 73.4 us  [the longest x1 70.8 us: on_device(): pl.pallas_call(functools.partial(kernel, nx, nz, ny), out_shape=shapes, i...]
where the time goes in v1:
time: 74.1 us; the launch traced here: 74 us
  Pallas kernels  73.4 us (99%)
    pallas_call x1, Pallas kernels, on_device(): pl.pallas_call(functools.partial(kernel, nx, nz, ny), out_shape=shapes, i...  70.8 us
    pallas_call x1, Pallas kernels, on_device(): pl.pallas_call(store_kernel, out_shape=shapes, in_specs=[vmem] * 7, out_s...  2.54 us

profile of v1, /device:TPU:1, one launch (start us, length us, event | category | flops | bytes accessed | tf_op | source)
XLA Modules:
  0.0 74.0 jit_solution(3622496617003693152)
XLA Ops:
  0.6 70.8 %shard_map.126 = (bf16[4,256,2048]{2,1,0:T(8,128)(2,1)S(1)}, f32[256,256]{1,0:T(8,128)S(1)}, f32[256,256]{1,0:T(8,128)S(1)}, f32[256,256]{1,0:T(8,128)S(1)}, f32...) custom-call(bf16[4,256,2048]{2,1,0:T(8,128)(2,1)} %bitcast.14, f32[256,256]{1,0:T(8,128)} %bitcast.15, ...), custom_call_target="tpu_custom_call" | custom-call | tf_op jit(solution)/shard_map/pallas_call | solution.py:333
  71.5 2.5 %shard_map.127 = (bf16[4,256,2048]{2,1,0:T(8,128)(2,1)}, f32[256,256]{1,0:T(8,128)}, f32[256,256]{1,0:T(8,128)}, f32[256,256]{1,0:T(8,128)}, f32[256,256]{1,0:T(...) custom-call(bf16[4,256,2048]{2,1,0:T(8,128)(2,1)S(1)} %get-tuple-element.21.refs_0_, ...), custom_call_target="tpu_custom_call" | custom-call | tf_op jit(solution)/shard_map/pallas_call | solution.py:364

commit v2 on v1

--- a/solution.py
+++ b/solution.py
@@ -12,8 +12,9 @@
 HI = lax.Precision.HIGHEST
 BLOCK = 256
 HALF = 128
+QUART = 64
 NB = 32
-EARLY = 3
+EARLY = 2
 
 beta_first = 0.9
 beta_second = 0.95
@@ -88,8 +89,9 @@
 def kernel(
     nx, nz, ny, part, mom, sec, lstat, rstat, lbas, rbas,
     upd, mom_o, sec_o, ln_o, rn_o, lb_o, rb_o,
-    state, own, r1, pair, rsib, r2, g_ref, tmp, wl, wr, nsend, nrecv,
-    s_state, s_own, s1s, s1r, sbs, sbr, s2s, s2r, nps, npr, a1s, a1r, a2s, a2r, abs_, abr,
+    state, own, f1, mid, msib, s2, r1, pair, rsib, f3, r2, g_ref, tmp, wl, wr, nsend, nrecv,
+    s_state, s_own, f1s, f1r, mss, msr, s2s, s2r, s1s, s1r, sbs, sbr, f3s, f3r, s3s, s3r,
+    nps, npr, a1s, a1r, a2s, a2r, abs_, abr,
 ):
     x, z, c, y = (lax.axis_index(a) for a in ("x", "z", "c", "y"))
     n = (nx, nz)
@@ -115,74 +117,127 @@
         for i, src in enumerate((mom, sec, lstat, rstat, lbas, rbas))
     ]
 
-    def slab(h, bx, bz):
-        return part.at[bx, HALF * h : HALF * (h + 1), pl.ds(pl.multiple_of(512 * bz, 512), 512)]
-
-    def chunk(h, d, e):
-        return slab(0, xs[d], zs[e]) if h == 0 else slab(1, xs[e], zs[d])
-
-    order = {h: [e for e in (2, 1, 3) if e < n[1 - h]] + [0] for h in (0, 1)}
-    dist = {h: [d for d in (2, 1, 3) if d < n[h]] for h in (0, 1)}
+    def chunk(h, d, e, r0=0, rows=HALF):
+        bx, bz = (xs[d], zs[e]) if h == 0 else (xs[e], zs[d])
+        r0 = HALF * h + r0
+        return part.at[bx, r0 : r0 + rows, pl.ds(pl.multiple_of(512 * bz, 512), 512)]
+
+    order = (2, 1, 3, 0)
+    ways = ((1, 0), (3, QUART))
     own_copies = {
-        (h, e): pltpu.make_async_copy(chunk(h, 0, e), own.at[h, e], s_own.at[h, e])
+        (h, e): [
+            pltpu.make_async_copy(src, own.at[h, e, at : at + rows], s_own.at[h, e])
+            for src, at, rows in (
+                (chunk(h, 0, e), 0, HALF),
+                (chunk(h, 1, e, 0, QUART), HALF, QUART),
+                (chunk(h, 3, e, QUART, QUART), HALF + QUART, QUART),
+            )
+        ]
+        for e in order
         for h in (0, 1)
-        for e in order[h]
     }
 
     barrier = pltpu.get_barrier_semaphore()
     hello = [peer(a, d) for a in (0, 1) for d in range(1, n[a])] + [(x, z, c, v) for v in ys[1:]] + [sib]
     for dev in hello:
         pl.semaphore_signal(barrier, inc=1, device_id=dev, device_id_type=MESH)
-    for q in own_copies.values():
-        q.start()
+    for e in order:
+        for h in (0, 1):
+            for q in own_copies[h, e]:
+                q.start()
     for q in loads:
         q.start()
     pl.semaphore_wait(barrier, len(hello))
 
-    for i in range(max(nx, nz)):
-        for h in (0, 1):
-            if i < len(order[h]):
-                e = order[h][i]
-                for d in dist[h]:
-                    rdma(chunk(h, d, e), r1.at[h, e, d - 1], s1s.at[0], s1r.at[h, e], peer(h, d)).start()
+    both = lambda f, *a: [f(h, *a) for h in (0, 1)]
+
+    def send_far(h, e):
+        for t, (d, r0) in enumerate(ways):
+            rdma(chunk(h, 2, e, r0, QUART), f1.at[h, e, t], f1s.at[0], f1r.at[h, e], peer(h, d)).start()
+
+    def send_near(h, e):
+        for t, (d, r0) in enumerate(ways):
+            rdma(chunk(h, d, e, QUART - r0, QUART), r1.at[h, e, t], s1s.at[0], s1r.at[h, e], peer(h, d)).start()
+
+    def add_far(h, e):
+        bytes_of(own.at[h, e], s_own.at[h, e])
+        bytes_of(f1.at[h, e], f1r.at[h, e])
+        for t in (0, 1):
+            at = HALF + QUART * t
+            total = own[h, e, at : at + QUART].astype(jnp.float32) + f1[h, e, t].astype(jnp.float32)
+            mid[h, e, 0, t] = total[:, :BLOCK]
+            mid[h, e, 1, t] = total[:, BLOCK:]
+        rdma(mid.at[h, e, cs[1]], msib.at[h, e], mss.at[0], msr.at[h, e], sib).start()
+
+    def send_sum(h, e):
+        bytes_of(msib.at[h, e], msr.at[h, e])
+        mid[h, e, c] = mid[h, e, c] + msib[h, e]
+        for t, (d, r0) in enumerate(ways):
+            rdma(mid.at[h, e, c, t], s2.at[h, e, t], s2s.at[0], s2r.at[h, e], peer(h, d)).start()
+
+    def add_near(h, e):
+        bytes_of(r1.at[h, e], s1r.at[h, e])
+        for t in (0, 1):
+            r0 = QUART * t
+            total = own[h, e, r0 : r0 + QUART].astype(jnp.float32) + r1[h, e, 1 - t].astype(jnp.float32)
+            pair[h, 0, e, t] = total[:, :BLOCK]
+            pair[h, 1, e, t] = total[:, BLOCK:]
+        rdma(pair.at[h, cs[1], e], rsib.at[h, e], sbs.at[0], sbr.at[h, e], sib).start()
+
+    def pass_on(h, e):
+        bytes_of(rsib.at[h, e], sbr.at[h, e])
+        bytes_of(s2.at[h, e], s2r.at[h, e])
+        pair[h, c, e] = pair[h, c, e] + (rsib[h, e] + s2[h, e])
+        if e == 2:
+            for t, (d, r0) in enumerate(ways):
+                rdma(pair.at[h, c, e, t], f3.at[h, t], f3s.at[0], f3r.at[h, t], peer(1 - h, d)).start()
+        elif e:
+            t = 0 if e == 1 else 1
+            bytes_of(f3.at[h, t], f3r.at[h, t])
+            pair[h, c, e, t] = pair[h, c, e, t] + f3[h, t]
+            rdma(pair.at[h, c, e], r2.at[h, t], s3s.at[0], s3r.at[h], peer(1 - h, e)).start()
+
+    for e in order:
+        both(send_far, e)
+    both(send_near, 2)
 
     for q in loads:
         q.wait()
     lb, rb = state[4], state[5]
     lbt, rbt = lb.T, rb.T
+    tmp[3] = lbt
+    tmp[4] = rbt
+
+    both(add_far, 2)
+    both(add_far, 1)
+    both(send_sum, 2)
+    both(send_near, 1)
+    both(add_far, 3)
+    both(send_sum, 1)
+    both(send_near, 3)
+    both(add_far, 0)
+    both(send_sum, 3)
+    both(send_near, 0)
+    both(send_sum, 0)
+
     tmp[0] = beta_second * mm(lbt, state[2])
     tmp[1] = beta_second * mm(rbt, state[3])
+    both(add_near, 2)
     tmp[2] = beta_first * mm(mm(lbt, state[0]), rb)
-    tmp[3] = lbt
-    tmp[4] = rbt
-
-    def pass_on(h, e):
-        bytes_of(rsib.at[h, e], sbr.at[h, e])
-        pair[h, c, e] = pair[h, c, e] + rsib[h, e]
-        if e:
-            rdma(pair.at[h, c, e], r2.at[h, e - 1], s2s.at[0], s2r.at[h], peer(1 - h, e)).start()
-
-    for i in range(max(nx, nz) + 1):
-        for h in (0, 1):
-            if i < len(order[h]):
-                e = order[h][i]
-                own_copies[h, e].wait()
-                bytes_of(r1.at[h, e], s1r.at[h, e])
-                total = own[h, e].astype(jnp.float32)
-                for d in range(1, n[h]):
-                    total = total + r1[h, e, d - 1].astype(jnp.float32)
-                pair[h, 0, e] = total[:, :BLOCK]
-                pair[h, 1, e] = total[:, BLOCK:]
-                rdma(pair.at[h, cs[1], e], rsib.at[h, e], sbs.at[0], sbr.at[h, e], sib).start()
-        for h in (0, 1):
-            if 1 <= i <= len(order[h]):
-                pass_on(h, order[h][i - 1])
+    both(pass_on, 2)
+    both(add_near, 1)
+    both(pass_on, 1)
+    both(add_near, 3)
+    both(pass_on, 3)
+    both(add_near, 0)
+    both(pass_on, 0)
     for h in (0, 1):
-        total = pair[h, c, 0]
-        bytes_of(r2.at[h], s2r.at[h])
-        for e in range(1, n[1 - h]):
-            total = total + r2[h, e - 1]
-        g_ref[HALF * h : HALF * (h + 1), :] = total
+        bytes_of(r2.at[h], s3r.at[h])
+        for t in (0, 1):
+            r0 = HALF * h + QUART * t
+            g_ref[r0 : r0 + QUART, :] = pair[h, c, 0, t] + (
+                r2[h, 0, t] + r2[h, 1, t]
+            )
 
     g = g_ref[...]
     gp, rbp = parts(g), parts(rb)
@@ -256,12 +311,12 @@
             send(spot(h, 0, s), a2s.at[0], a2r.at[h, d - 1, s], peer(h, d))
         share(h, 0, s)
 
-    ways = {0: 1, 1: 3, 3: 1}
+    relayed = {0: 1, 1: 3, 3: 1}
 
     def relay(h, s):
         for d in (1, 3):
             arrive(spot(h, d, s), a2r.at[h, d - 1, s])
-            if ways.get(s) == d:
+            if relayed.get(s) == d:
                 send(spot(h, d, s), a2s.at[0], a2r.at[h, 1, s], peer(h, d))
             share(h, d, s)
 
@@ -269,7 +324,6 @@
         arrive(spot(h, 2, s), a2r.at[h, 1, s])
         share(h, 2, s)
 
-    both = lambda f, *a: [f(h, *a) for h in (0, 1)]
     both(start)
     both(onward, 0)
 
@@ -300,9 +354,9 @@
             both(*q)
 
     bytes_of(upd.at[0:2], abr.at[0])
-    bytes_of(r1, s1s.at[0])
-    bytes_of(rsib, sbs.at[0])
-    bytes_of(r2, s2s.at[0])
+    for ref, sem in ((f1, f1s), (msib, mss), (s2, s2s), (r1, s1s), (rsib, sbs), (f3, f3s)):
+        bytes_of(ref, sem.at[0])
+    bytes_of(r2, s3s.at[0])
     bytes_of(nrecv.at[0:others, :], nps.at[0])
     bytes_of(upd.at[0, 0:192, 0:1024], a1s.at[0])
     bytes_of(upd.at[0:3, 0:128, :], a2s.at[0])
@@ -337,11 +391,16 @@
         out_specs=[vmem] * 7,
         scratch_shapes=[
             pltpu.VMEM((6, *square), f32),
-            pltpu.VMEM((2, ring, HALF, 2 * BLOCK), bf16),
-            pltpu.VMEM((2, ring, ring - 1, HALF, 2 * BLOCK), bf16),
-            pltpu.VMEM((2, 2, ring, HALF, BLOCK), f32),
-            pltpu.VMEM((2, ring, HALF, BLOCK), f32),
-            pltpu.VMEM((2, ring - 1, HALF, BLOCK), f32),
+            pltpu.VMEM((2, ring, BLOCK, 2 * BLOCK), bf16),
+            pltpu.VMEM((2, ring, 2, QUART, 2 * BLOCK), bf16),
+            pltpu.VMEM((2, ring, 2, 2, QUART, BLOCK), f32),
+            pltpu.VMEM((2, ring, 2, QUART, BLOCK), f32),
+            pltpu.VMEM((2, ring, 2, QUART, BLOCK), f32),
+            pltpu.VMEM((2, ring, 2, QUART, 2 * BLOCK), bf16),
+            pltpu.VMEM((2, 2, ring, 2, QUART, BLOCK), f32),
+            pltpu.VMEM((2, ring, 2, QUART, BLOCK), f32),
+            pltpu.VMEM((2, 2, QUART, BLOCK), f32),
+            pltpu.VMEM((2, 2, 2, QUART, BLOCK), f32),
             pltpu.VMEM(square, f32),
             pltpu.VMEM((5, *square), f32),
             pltpu.VMEM((BLOCK, 2 * BLOCK), f32),
@@ -351,6 +410,10 @@
             dma((6,)), dma((2, ring)),
             dma((1,)), dma((2, ring)),
             dma((1,)), dma((2, ring)),
+            dma((1,)), dma((2, ring)),
+            dma((1,)), dma((2, ring)),
+            dma((1,)), dma((2, ring)),
+            dma((1,)), dma((2, 2)),
             dma((1,)), dma((2,)),
             dma((1,)), dma((1,)),
             dma((1,)), dma((2, ring - 1)),

time: 74.1 us -> 68.7 us (0.927)
  Pallas kernels: 73.4 us -> 67.9 us
    pallas_call x1, Pallas kernels: 70.8 us -> 65.4 us  [on_device(): pl.pallas_call(functools.partial(kernel, nx, nz, ny), out_shape=shapes, i...]
where the time goes in v2:
time: 68.7 us; the launch traced here: 68.6 us
  Pallas kernels  67.9 us (99%)
    pallas_call x1, Pallas kernels, on_device(): pl.pallas_call(functools.partial(kernel, nx, nz, ny), out_shape=shapes, i...  65.4 us
    pallas_call x1, Pallas kernels, on_device(): pl.pallas_call(store_kernel, out_shape=shapes, in_specs=[vmem] * 7, out_s...  2.54 us

profile of v2, /device:TPU:1, one launch (start us, length us, event | category | flops | bytes accessed | tf_op | source)
XLA Modules:
  0.0 68.6 jit_solution(14794718955638758204)
XLA Ops:
  0.6 65.4 %shard_map.126 = (bf16[4,256,2048]{2,1,0:T(8,128)(2,1)S(1)}, f32[256,256]{1,0:T(8,128)S(1)}, f32[256,256]{1,0:T(8,128)S(1)}, f32[256,256]{1,0:T(8,128)S(1)}, f32...) custom-call(bf16[4,256,2048]{2,1,0:T(8,128)(2,1)} %bitcast.14, f32[256,256]{1,0:T(8,128)} %bitcast.15, ...), custom_call_target="tpu_custom_call" | custom-call | tf_op jit(solution)/shard_map/pallas_call | solution.py:387
  66.0 2.5 %shard_map.127 = (bf16[4,256,2048]{2,1,0:T(8,128)(2,1)}, f32[256,256]{1,0:T(8,128)}, f32[256,256]{1,0:T(8,128)}, f32[256,256]{1,0:T(8,128)}, f32[256,256]{1,0:T(...) custom-call(bf16[4,256,2048]{2,1,0:T(8,128)(2,1)S(1)} %get-tuple-element.21.refs_0_, ...), custom_call_target="tpu_custom_call" | custom-call | tf_op jit(solution)/shard_map/pallas_call | solution.py:427
